TPU v7x, 32 devices: a whole 2x2x4 slice. The times are simulated.
32 devices in a mesh: groups: 2 (over y), seq: 4 (over z), exp: 2 (over x), tp: 2 (over core).
Axes of the slice: x: 2, y: 2, z: 4, core: 2. Of those that a mesh axis runs over, the one named last changes fastest.
Arguments:
- attn_query: bfloat16 [2048, 1152], P(('groups', 'seq'), ('exp', 'tp')), parts along dimension 0, may hold values from -6 to 6
- fresh_keys: bfloat16 [2048, 1152], P(('groups', 'seq'), ('exp', 'tp')), parts along dimension 0, may hold values from -6 to 6
- fresh_values: bfloat16 [2048, 1152], P(('groups', 'seq'), ('exp', 'tp')), parts along dimension 0, may hold values from -6 to 6
- stale_keys: bfloat16 [2048, 1152], P(('groups', 'seq'), ('exp', 'tp')), parts along dimension 0, may hold values from -6 to 6
- stale_values: bfloat16 [2048, 1152], P(('groups', 'seq'), ('exp', 'tp')), parts along dimension 0, may hold values from -6 to 6
- block_flags: int32 [16], P(('groups', 'seq')), parts along dimension 0, may hold values 0 or 1
- moe_tokens: bfloat16 [4096, 1152], P(('groups', 'seq', 'exp', 'tp')), parts along dimension 0, may hold values from -6 to 6
- expert_ids: int32 [4096, 2], P(('groups', 'seq', 'exp', 'tp')), parts along dimension 0, may hold values from 0 to 3, all different within a row; in each aligned block of 128 rows (0 to 127, 128 to 255, ...) at most 80 rows name the same one
- gate_weights: float32 [4096, 2], P(('groups', 'seq', 'exp', 'tp')), parts along dimension 0, may hold values from 0.25 to 1
- up_weight: bfloat16 [4, 1152, 4608], P('seq', None, ('exp', 'tp')), may hold values from -0.1875 to 0.1875
- up_bias: float32 [4, 4608], P('seq', ('exp', 'tp')), may hold values from -3 to 3
- down_weight: bfloat16 [4, 4608, 1152], P('seq', ('exp', 'tp')), may hold values from -0.09375 to 0.09375
- down_bias: float32 [4, 1152], P('seq'), may hold values from -2 to 2
Outputs:
- attn_out: bfloat16 [2048, 1152], P(('groups', 'seq'), ('exp', 'tp')), parts along dimension 0
- moe_out: bfloat16 [4096, 1152], P(('groups', 'seq', 'exp', 'tp')), parts along dimension 0
There are 2 independent parts, one for each index of `groups`. A program takes and returns all parts, laid end to end along the dimension named above; an argument that names none is the same for every part. Nothing has to cross between parts.
Inputs may be any that keep to these rules, and one draw needn't show every extreme that they name: `expert_ids`: the 2 ids of a token differ. In the rows of one device no expert is named more than 80 times, and in every draw some expert is named exactly 80 times in some device's rows.
All inputs are finite; a program needn't handle non-finite values. No bound on the sum of `block_flags` on one device may be relied on, other than what follows from the above.
Results may differ from a plain program's by a relative error of at most 0.014.
Values may be sent and summed in bfloat16 or wider, within the bound.
A program may use at most 64 MiB of HBM per device.

v0:
```python
import math

import jax
import jax.numpy as jnp
from jax import lax
from jax.sharding import PartitionSpec as P

HD = 72


def over_all_2(share, axis, dim, apply):
    everything = lax.all_gather(share, axis, axis=dim, tiled=True)
    return apply(everything, jnp.int32(0))


def attention_part(attn_query, fresh_keys, fresh_values, stale_keys, stale_values, block_flags):
    length = attn_query.shape[0]
    heads_here = attn_query.shape[1] // HD
    row_flags = (jnp.repeat(block_flags, length // block_flags.shape[0]) == 1)[:, None]
    keys = jnp.where(row_flags, fresh_keys, stale_keys)
    values = jnp.where(row_flags, fresh_values, stale_values)
    queries = attn_query.reshape(length, heads_here, HD)
    scale = 1.0 / math.sqrt(HD)
    initial = (
        jnp.full((heads_here, length), -1e30, jnp.float32),
        jnp.zeros((heads_here, length), jnp.float32),
        jnp.zeros((heads_here, length, HD), jnp.float32),
    )
    carry = initial
    piece = (
        lax.all_gather(keys, "seq", axis=0, tiled=True),
        lax.all_gather(values, "seq", axis=0, tiled=True),
    )
    count = piece[0].shape[0]
    width = math.gcd(count, 512)
    key_blocks = piece[0].reshape(count // width, width, heads_here, HD)
    value_blocks = piece[1].reshape(count // width, width, heads_here, HD)

    def advance(state, blocks):
        highest, totals, weighted = state
        key_block, value_block = blocks
        scores = (
            jnp.einsum("qhd,khd->hqk", queries, key_block, preferred_element_type=jnp.float32)
            * scale
        )
        new_high = jnp.maximum(highest, jnp.max(scores, axis=-1))
        rescale = jnp.exp(highest - new_high)
        probs = jnp.exp(scores - new_high[:, :, None])
        totals = totals * rescale + jnp.sum(probs, axis=-1)
        weighted = weighted * rescale[:, :, None] + jnp.einsum(
            "hqk,khd->hqd",
            probs.astype(jnp.bfloat16),
            value_block,
            preferred_element_type=jnp.float32,
        )
        return ((new_high, totals, weighted), None)

    carry, unused = lax.scan(advance, carry, (key_blocks, value_blocks))
    highest, totals, weighted = carry
    mixed = weighted / totals[:, :, None]
    return jnp.transpose(mixed, (1, 0, 2)).reshape(length, heads_here * HD).astype(jnp.bfloat16)


def expert_part(moe_tokens, expert_ids, gate_weights, up_weight, up_bias, down_weight, down_bias):
    tokens_here, width = moe_tokens.shape
    choose = expert_ids.shape[1]
    number = lax.axis_size("seq") * up_weight.shape[0]
    capacity = 5 * tokens_here // (2 * number)
    flat_ids = expert_ids.reshape(-1)
    hits = (flat_ids[:, None] == jnp.arange(number, dtype=jnp.int32)[None, :]).astype(jnp.int32)
    before = jnp.cumsum(hits, axis=0) - hits
    place = jnp.sum(before * hits, axis=1)
    slot = flat_ids * capacity + place
    slot_pairs = slot.reshape(tokens_here, choose)
    table = jnp.sum(
        (
            slot_pairs[None, :, :] == jnp.arange(number * capacity, dtype=jnp.int32)[:, None, None]
        ).astype(jnp.int32),
        axis=-1,
    )
    buffer = jnp.dot(
        table.astype(jnp.bfloat16), moe_tokens, preferred_element_type=jnp.float32
    ).astype(jnp.bfloat16)
    buffer = buffer.reshape(number, capacity, width)
    received = lax.all_to_all(buffer, "seq", split_axis=0, concat_axis=0, tiled=True)
    sources = received.shape[0]
    count = received.shape[1]
    flat_rows = received.reshape(sources * count, width)
    chip_rows = lax.all_gather(flat_rows, "tp", axis=0, tiled=True)

    def project(piece):
        return jax.nn.gelu(
            jnp.dot(chip_rows, piece[0], preferred_element_type=jnp.float32) + piece[1]
        ).astype(jnp.bfloat16)

    hidden = over_all_2(
        (up_weight[0], up_bias[0][None, :].astype(jnp.bfloat16)),
        "exp",
        1,
        lambda piece, start: project((piece[0], piece[1].astype(jnp.float32))),
    )
    down_whole = lax.all_gather(down_weight[0], "exp", axis=0, tiled=True)
    summed = lax.psum_scatter(
        jnp.dot(hidden, down_whole, preferred_element_type=jnp.float32).astype(jnp.bfloat16),
        "tp",
        scatter_dimension=0,
        tiled=True,
    ).astype(jnp.float32)
    result = (summed + down_bias[0][None, :]).astype(jnp.bfloat16).reshape(sources, count, width)
    returned = lax.all_to_all(result, "seq", split_axis=0, concat_axis=0, tiled=True)
    flat_out = returned.reshape(number * capacity, width)
    picked = flat_out[slot].reshape(tokens_here, choose, width).astype(jnp.float32)
    combined = jnp.sum(picked * gate_weights[:, :, None], axis=1)
    return combined.astype(jnp.bfloat16)


def local(
    attn_query,
    fresh_keys,
    fresh_values,
    stale_keys,
    stale_values,
    block_flags,
    moe_tokens,
    expert_ids,
    gate_weights,
    up_weight,
    up_bias,
    down_weight,
    down_bias,
):
    attn_out = attention_part(
        attn_query, fresh_keys, fresh_values, stale_keys, stale_values, block_flags
    )
    moe_out = expert_part(
        moe_tokens, expert_ids, gate_weights, up_weight, up_bias, down_weight, down_bias
    )
    return (attn_out, moe_out)


def solution(mesh):
    in_specs = (
        P(("groups", "seq"), ("exp", "tp")),
        P(("groups", "seq"), ("exp", "tp")),
        P(("groups", "seq"), ("exp", "tp")),
        P(("groups", "seq"), ("exp", "tp")),
        P(("groups", "seq"), ("exp", "tp")),
        P(("groups", "seq")),
        P(("groups", "seq", "exp", "tp"), None),
        P(("groups", "seq", "exp", "tp"), None),
        P(("groups", "seq", "exp", "tp"), None),
        P("seq", None, ("exp", "tp")),
        P("seq", ("exp", "tp")),
        P("seq", ("exp", "tp"), None),
        P("seq", None),
    )
    out_specs = (P(("groups", "seq"), ("exp", "tp")), P(("groups", "seq", "exp", "tp"), None))
    return jax.shard_map(local, mesh=mesh, in_specs=in_specs, out_specs=out_specs, check_vma=False)
```

profile of v0, /device:TPU:0, one launch (start us, length us, event | category | flops | bytes accessed | tf_op | source)
XLA Modules:
  0.0 262.1 jit_solution(10440550585438227936)
XLA Ops:
  7.2 0.8 copy.32
  8.3 1.2 reduce-window.6
  10.3 0.3 convolution_convert_fusion
  10.6 25.3 %all_to_all.10 = bf16[4,80,1152]{2,1,0:T(8,128)(2,1)} all-to-all(bf16[4,80,1152]{2,1,0:T(8,128)(2,1)S(1)} %bitcast.82), channel_id=1, replica_groups=mesh['groups'=2,'seq'=4,'exp'=2,'tp'=2] {'seq'}, dimensions={0} | all-to-all | bytes 1474560 | tf_op jit(solution)/shard_map/all_to_all | solution.py:85
  36.0 0.7 all-gather.8.cloned.1.call-update
  36.8 0.7 all-gather.10.cloned.1.call-update
  37.5 4.4 %all_gather.22 = bf16[1,2304]{1,0:T(2,128)(2,1)S(1)} all-gather(bf16[1,1152]{1,0:T(2,128)(2,1)S(1)} %convert_element_type.61), channel_id=1, replica_groups=mesh['groups'=2,'seq'=4,'exp'=2,'tp'=2] {'exp'}, dimensions={1}, use_global_device_ids=true | all-gather | bytes 6912 | tf_op jit(solution)/shard_map/all_gather | solution.py:12
  41.9 3.0 %all-gather.6.cloned.1.call-done = bf16[640,1152]{1,0:T(8,128)(2,1)} async-done(((bf16[320,1152]{1,0:T(8,128)(2,1)}), bf16[640,1152]{1,0:T(8,128)(2,1)}) %all-gather.6.cloned.1.call-update) | async-done | bytes 1474576 | tf_op jit(solution)/shard_map/all_gather | solution.py:89
  44.9 72.0 %all-gather.8.cloned.1.call-done = bf16[1,1152,2304]{2,1,0:T(8,128)(2,1)} async-done(((bf16[1,1152,1152]{2,1,0:T(8,128)(2,1)}), bf16[1,1152,2304]{2,1,0:T(8,128)(2,1)}) %all-gather.8.cloned.1.call-update) | async-done | bytes 5308432 | tf_op jit(solution)/shard_map/all_gather | solution.py:12
  116.9 9.6 %fusion.22 = bf16[640,2304]{1,0:T(8,128)(2,1)} fusion(bf16[640,1152]{1,0:T(8,128)(2,1)} %all-gather.6.cloned.1.call-done, bf16[1,1152,2304]{2,1,0:T(8,128)(2,1)} %all-gather.8.cloned.1.call-done, f32[2304]{0:T(1024)S(1)} %convert_reduce_fusion.1), kind=kOutput, calls=%fused_computation.30 | convolution fusion | flops 3412131840 | bytes 9741312 | tf_op jit(solution)/shard_map/dot_general | solution.py:93
  126.5 61.3 %all-gather.10.cloned.1.call-done = bf16[1,2304,1152]{2,1,0:T(8,128)(2,1)} async-done(((bf16[1,1152,1152]{2,1,0:T(8,128)(2,1)}), bf16[1,2304,1152]{2,1,0:T(8,128)(2,1)}) %all-gather.10.cloned.1.call-update) | async-done | bytes 5308432 | tf_op jit(solution)/shard_map/all_gather | solution.py:102
  187.8 8.5 %fusion.29 = bf16[640,1152]{1,0:T(8,128)(2,1)} fusion(bf16[640,2304]{1,0:T(8,128)(2,1)} %fusion.22, bf16[1,2304,1152]{2,1,0:T(8,128)(2,1)} %all-gather.10.cloned.1.call-done), kind=kOutput, calls=%fused_computation.35 | convolution fusion | flops 3398123520 | bytes 9732096 | tf_op jit(solution)/shard_map/dot_general | solution.py:104
  196.5 16.5 %all_gather.18 = bf16[1024,288]{0,1:T(8,128)(2,1)S(1)} all-gather(bf16[256,288]{0,1:T(8,128)(2,1)S(1)} %get-tuple-element.101), channel_id=1, replica_groups=mesh['groups'=2,'seq'=4,'exp'=2,'tp'=2] {'seq'}, dimensions={0}, use_global_device_ids=true | all-gather | bytes 737280 | tf_op jit(solution)/shard_map/all_gather | solution.py:31
  213.1 0.4 reshape.94
  213.5 0.9 copy.30
  214.4 16.1 %all_gather.19 = bf16[1024,288]{0,1:T(8,128)(2,1)S(1)} all-gather(bf16[256,288]{0,1:T(8,128)(2,1)S(1)} %get-tuple-element.100), channel_id=1, replica_groups=mesh['groups'=2,'seq'=4,'exp'=2,'tp'=2] {'seq'}, dimensions={0}, use_global_device_ids=true | all-gather | bytes 737280 | tf_op jit(solution)/shard_map/all_gather | solution.py:32
  230.5 0.4 reshape.96
  230.9 0.9 copy.31
  231.9 2.1 add_convert_fusion
  234.0 4.9 %all-to-all-start.1 = ((bf16[4,80,1152]{2,1,0:T(8,128)(2,1)}), bf16[4,80,1152]{2,1,0:T(8,128)(2,1)S(1)}, u32[]{:S(2)}, u32[]{:S(2)}) async-start(bf16[4,80,1152]{2,1,0:T(8,128)(2,1)} %bitcast.10), calls=%async_computation.2 | async-start | bytes 1474560 | tf_op jit(solution)/shard_map/all_to_all | solution.py:110
  238.8 6.9 %while.15 = (s32[]{:T(128)}, f32[4,256]{1,0:T(4,128)S(1)}, f32[4,256]{1,0:T(4,128)S(1)}, f32[4,256,72]{1,2,0:T(8,128)S(1)}, bf16[2,512,4,72]{1,3,2,0:T(8,128)(2,...) while((s32[]{:T(128)}, f32[4,256]{1,0:T(4,128)S(1)}, ...), condition=%wide.region_3.4_spmd.clone, body=%wide.region_0.3_spmd.clone.sunk | while | flops 155415552 | bytes 7685225 | solution.py:58
  238.8 1.5 bitcast_reduce_fusion.2
  240.4 0.4 fusion.49
  240.8 1.5 convolution_add_fusion.2
  242.3 1.5 bitcast_reduce_fusion.2
  243.8 0.4 fusion.49
  244.2 1.5 convolution_add_fusion.2
  246.0 0.7 divide_convert_fusion
  246.7 4.9 %all-to-all-done.1 = bf16[4,80,1152]{2,1,0:T(8,128)(2,1)S(1)} async-done(((bf16[4,80,1152]{2,1,0:T(8,128)(2,1)}), bf16[4,80,1152]{2,1,0:T(8,128)(2,1)S(1)}, u32[]{:S(2)}, u32[]{:S(2)}) %all-to-all-start.1) | async-done | bytes 737312 | tf_op jit(solution)/shard_map/all_to_all | solution.py:110
  251.6 1.3 gather_fusion
  252.8 0.6 reshape.103
  253.4 2.2 multiply_reduce_fusion
  (58 shorter events, 1.7 us)
Async XLA Ops:
  7.2 3.1 %copy-start = (bf16[128,1152]{1,0:T(8,128)(2,1)S(1)}, bf16[128,1152]{1,0:T(8,128)(2,1)}, u32[]{:S(2)}) copy-start(bf16[128,1152]{1,0:T(8,128)(2,1)} %param.21) | copy-start | bytes 884740
  7.2 37.7 %all-gather.6.cloned.1.call-start = ((), (), s32[]{:S(2)}) async-start(), calls=%async_computation.3 | async-start | bytes 2211840 | tf_op jit(solution)/shard_map/all_gather | solution.py:89
  36.0 1.5 copy-start.5
  36.0 80.9 %all-gather.8.cloned.1.call-start = ((), (), s32[]{:S(2)}) async-start(), calls=%async_computation.5 | async-start | bytes 7962624 | tf_op jit(solution)/shard_map/all_gather | solution.py:12
  36.7 151.0 %all-gather.10.cloned.1.call-start = ((), (), s32[]{:S(2)}) async-start(), calls=%async_computation.6 | async-start | bytes 7962624 | tf_op jit(solution)/shard_map/all_gather | solution.py:102
  37.5 194.4 %reduce-scatter.2.cloned.1.call-start = ((), (), s32[]{:S(2)}) async-start(), calls=%async_computation.4 | async-start | bytes 2211840 | tf_op jit(solution)/shard_map/reduce_scatter | solution.py:103
  126.5 69.9 %copy-start.8 = (s32[2]{0:T(128)S(1)}, s32[2]{0:T(128)}, u32[]{:S(2)}) copy-start(s32[2]{0:T(128)} %param.20) | copy-start | bytes 28
  126.5 70.0 %copy-start.1 = (bf16[256,288]{0,1:T(8,128)(2,1)S(1)}, bf16[256,288]{0,1:T(8,128)(2,1)}, u32[]{:S(2)}) copy-start(bf16[256,288]{0,1:T(8,128)(2,1)} %param.17) | copy-start | bytes 442372
  126.5 70.0 %copy-start.2 = (bf16[256,288]{0,1:T(8,128)(2,1)S(1)}, bf16[256,288]{0,1:T(8,128)(2,1)}, u32[]{:S(2)}) copy-start(bf16[256,288]{0,1:T(8,128)(2,1)} %param.19) | copy-start | bytes 442372
  126.5 70.0 %copy-start.3 = (bf16[256,288]{0,1:T(8,128)(2,1)S(1)}, bf16[256,288]{0,1:T(8,128)(2,1)}, u32[]{:S(2)}) copy-start(bf16[256,288]{0,1:T(8,128)(2,1)} %param.16) | copy-start | bytes 442372
  126.5 70.0 %copy-start.4 = (bf16[256,288]{0,1:T(8,128)(2,1)S(1)}, bf16[256,288]{0,1:T(8,128)(2,1)}, u32[]{:S(2)}) copy-start(bf16[256,288]{0,1:T(8,128)(2,1)} %param.18) | copy-start | bytes 442372
  213.1 18.7 %copy-start.6 = (f32[1,1152]{1,0:T(1,128)S(1)}, f32[1,1152]{1,0:T(1,128)}, u32[]{:S(2)}) copy-start(f32[1,1152]{1,0:T(1,128)} %param.27) | copy-start | bytes 13828
  234.0 17.6 %all-to-all-start.1 = ((bf16[4,80,1152]{2,1,0:T(8,128)(2,1)}), bf16[4,80,1152]{2,1,0:T(8,128)(2,1)S(1)}, u32[]{:S(2)}, u32[]{:S(2)}) async-start(bf16[4,80,1152]{2,1,0:T(8,128)(2,1)} %bitcast.10), calls=%async_computation.2 | async-start | bytes 1474560 | tf_op jit(solution)/shard_map/all_to_all | solution.py:110
  238.8 7.0 %copy-start.7 = (f32[128,2]{0,1:T(2,128)S(1)}, f32[128,2]{0,1:T(2,128)}, u32[]{:S(2)}) copy-start(f32[128,2]{0,1:T(2,128)} %param.23) | copy-start | bytes 3076
Sparse Core Ops, SparseCore 0:
  36.1 8.7 all-gather.5
  46.4 70.4 all-gather.7
  118.5 69.2 all-gather.9
  196.5 8.9 reduce-scatter.1
where the time goes:
time: 263 us; the launch traced here: 262 us
  waiting for transfers between devices  143 us (54%)
  blocking collectives  62.3 us (24%)
  matrix products  24.4 us (9%)
  between operations  14 us (5%)
  other arithmetic  7.3 us (3%)
  local copies, waits for them, and re-layouts  6.41 us (2%)
  starting transfers between devices  5.02 us (2%)
    all_gather x1, waiting for transfers between devices, over_all_2(): everything = lax.all_gather(share, axis, axis=dim, tiled=True)  72 us
    all_gather x1, waiting for transfers between devices, expert_part(): down_whole = lax.all_gather(down_weight[0], 'exp', axis=0, tiled=True)  61.3 us
    all_to_all x1, blocking collectives, expert_part(): lax.all_to_all(buffer, 'seq', split_axis=0, concat_axis=0, tiled=True)  25.3 us
    all_gather x1, blocking collectives, attention_part(): lax.all_gather(keys, 'seq', axis=0, tiled=True)  16.5 us
    all_gather x1, blocking collectives, attention_part(): lax.all_gather(values, 'seq', axis=0, tiled=True)  16.1 us
    dot_general x1, matrix products, project(): jnp.dot(chip_rows, piece[0], preferred_element_type=jnp.float32) + piece[1]  9.57 us
    dot_general x1, matrix products, expert_part(): jnp.dot(hidden, down_whole, preferred_element_type=jnp.float32)  8.54 us
  transfers between devices with their start and end apart: 5, of which 4 were waited for; matrix products, arithmetic and copies ran while one was open for 8% of the time, Pallas kernels for 0%

commit v1 on v0

--- a/solution.py
+++ b/solution.py
@@ -6,11 +6,6 @@
 from jax.sharding import PartitionSpec as P
 
 HD = 72
-
-
-def over_all_2(share, axis, dim, apply):
-    everything = lax.all_gather(share, axis, axis=dim, tiled=True)
-    return apply(everything, jnp.int32(0))
 
 
 def attention_part(attn_query, fresh_keys, fresh_values, stale_keys, stale_values, block_flags):
@@ -27,10 +22,8 @@
         jnp.zeros((heads_here, length, HD), jnp.float32),
     )
     carry = initial
-    piece = (
-        lax.all_gather(keys, "seq", axis=0, tiled=True),
-        lax.all_gather(values, "seq", axis=0, tiled=True),
-    )
+    both = lax.all_gather(jnp.concatenate([keys, values], axis=1), "seq", axis=0, tiled=True)
+    piece = (both[:, : keys.shape[1]], both[:, keys.shape[1] :])
     count = piece[0].shape[0]
     width = math.gcd(count, 512)
     key_blocks = piece[0].reshape(count // width, width, heads_here, HD)
@@ -86,23 +79,13 @@
     sources = received.shape[0]
     count = received.shape[1]
     flat_rows = received.reshape(sources * count, width)
-    chip_rows = lax.all_gather(flat_rows, "tp", axis=0, tiled=True)
-
-    def project(piece):
-        return jax.nn.gelu(
-            jnp.dot(chip_rows, piece[0], preferred_element_type=jnp.float32) + piece[1]
-        ).astype(jnp.bfloat16)
-
-    hidden = over_all_2(
-        (up_weight[0], up_bias[0][None, :].astype(jnp.bfloat16)),
-        "exp",
-        1,
-        lambda piece, start: project((piece[0], piece[1].astype(jnp.float32))),
-    )
-    down_whole = lax.all_gather(down_weight[0], "exp", axis=0, tiled=True)
+    chip_rows = lax.all_gather(flat_rows, ("exp", "tp"), axis=0, tiled=True)
+    hidden = jax.nn.gelu(
+        jnp.dot(chip_rows, up_weight[0], preferred_element_type=jnp.float32) + up_bias
+    ).astype(jnp.bfloat16)
     summed = lax.psum_scatter(
-        jnp.dot(hidden, down_whole, preferred_element_type=jnp.float32).astype(jnp.bfloat16),
-        "tp",
+        jnp.dot(hidden, down_weight[0], preferred_element_type=jnp.float32).astype(jnp.bfloat16),
+        ("exp", "tp"),
         scatter_dimension=0,
         tiled=True,
     ).astype(jnp.float32)

time: 263 us -> 176 us (0.67)
  waiting for transfers between devices: 143 us -> 76.8 us
  blocking collectives: 62.3 us -> 25.3 us
  local copies, waits for them, and re-layouts: 6.41 us -> 16.9 us
  other arithmetic: 7.3 us -> 13.8 us
    all_gather x3 -> x2, waiting for transfers between devices: 136 us -> 45.1 us  [the longest x1 25.6 us: expert_part(): chip_rows = lax.all_gather(flat_rows, ('exp', 'tp'), axis=0, tiled=True)]
    all_gather x3 -> x0, blocking collectives: 37 us -> none  [the longest x1 16.5 us: attention_part(): lax.all_gather(keys, 'seq', axis=0, tiled=True)]
    reduce_scatter x1, waiting for transfers between devices: 0.02 us -> 28.8 us  [expert_part(): lax.psum_scatter(jnp.dot(hidden, down_weight[0], preferred_element_type=j...]
    dot_general x2 -> x1, matrix products: 18.1 us -> 12.3 us  [expert_part(): jnp.dot(hidden, down_weight[0], preferred_element_type=jnp.float32)]
    reduce_sum x2, other arithmetic: 0.73 us -> 4.2 us  [advance(): totals = totals * rescale + jnp.sum(probs, axis=-1)]
  transfers between devices with their start and end apart: 5 -> 4, of which waited for: 4 -> 4; matrix products, arithmetic and copies ran while one was open for 8% -> 22% of each run, Pallas kernels for 0% -> 0%
where the time goes in v1:
time: 176 us; the launch traced here: 175 us
  waiting for transfers between devices  76.8 us (44%)
  blocking collectives  25.3 us (14%)
  matrix products  23.6 us (13%)
  local copies, waits for them, and re-layouts  16.9 us (10%)
  between operations  14 us (8%)
  other arithmetic  13.8 us (8%)
  starting transfers between devices  4.73 us (3%)
    reduce_scatter x1, waiting for transfers between devices, expert_part(): lax.psum_scatter(jnp.dot(hidden, down_weight[0], preferred_element_type=j...  28.8 us
    all_gather x1, waiting for transfers between devices, expert_part(): chip_rows = lax.all_gather(flat_rows, ('exp', 'tp'), axis=0, tiled=True)  25.6 us
    all_to_all x1, blocking collectives, expert_part(): lax.all_to_all(buffer, 'seq', split_axis=0, concat_axis=0, tiled=True)  25.3 us
    all_gather x1, waiting for transfers between devices, attention_part(): lax.all_gather(jnp.concatenate([keys, values], axis=1), 'seq', axis=0, ti...  19.5 us
    dot_general x1, matrix products, expert_part(): jnp.dot(hidden, down_weight[0], preferred_element_type=jnp.float32)  12.3 us
    dot_general x2, matrix products, advance(): jnp.einsum('qhd,khd->hqk', queries, key_block, preferred_element_type=jnp...  5.61 us
    all_to_all x1, starting transfers between devices, expert_part(): lax.all_to_all(result, 'seq', split_axis=0, concat_axis=0, tiled=True)  4.61 us
    dot_general x2, matrix products, advance(): jnp.einsum('hqk,khd->hqd', probs.astype(jnp.bfloat16), value_block, prefe...  4.39 us
  transfers between devices with their start and end apart: 4, of which 4 were waited for; matrix products, arithmetic and copies ran while one was open for 22% of the time, Pallas kernels for 0%

profile of v1, /device:TPU:0, one launch (start us, length us, event | category | flops | bytes accessed | tf_op | source)
XLA Modules:
  0.0 175.1 jit_solution(16136607486780483135)
XLA Ops:
  7.3 0.9 copy.32
  8.4 0.1 eq.55
  8.5 1.2 reduce-window.6
  10.2 0.1 reduce_sum.41
  10.4 1.3 convolution_convert_fusion.1
  11.8 25.3 %all_to_all.10 = bf16[4,80,1152]{2,1,0:T(8,128)(2,1)} all-to-all(bf16[4,80,1152]{2,1,0:T(8,128)(2,1)S(1)} %bitcast.80), channel_id=1, replica_groups=mesh['groups'=2,'seq'=4,'exp'=2,'tp'=2] {'seq'}, dimensions={0} | all-to-all | bytes 1474560 | tf_op jit(solution)/shard_map/all_to_all | solution.py:78
  37.3 0.8 pad_maximum_fusion
  38.2 25.6 %all-gather.5.cloned.1.call-done = bf16[1280,1152]{1,0:T(8,128)(2,1)} async-done(((bf16[320,1152]{1,0:T(8,128)(2,1)}), bf16[1280,1152]{1,0:T(8,128)(2,1)}) %all-gather.5.cloned.1.call-update) | async-done | bytes 2949136 | tf_op jit(solution)/shard_map/all_gather | solution.py:82
  63.7 12.3 %convolution_convert_fusion = bf16[1280,1152]{1,0:T(8,128)(2,1)} fusion(bf16[1,1152,1152]{2,1,0:T(8,128)(2,1)S(1)} %copy-done, bf16[1280,1152]{1,0:T(8,128)(2,1)} %all-gather.5.cloned.1.call-done, f32[1152]{0:T(1024)S(1)} %reduce, bf16[1,1152,1152]{2,1,0:T(8,128)(2,1)} %param.24), kind=kOutput, calls=%fused_computation.24 | convolution fusion | flops 6810992640 | bytes 11211264 | tf_op jit(solution)/shard_map/dot_general | solution.py:87
  76.2 0.5 copy-done.9
  76.8 0.7 copy.38
  77.5 19.5 %all-gather.3.cloned.1.call-done = bf16[1024,576]{0,1:T(8,128)(2,1)} async-done(((bf16[256,576]{0,1:T(8,128)(2,1)}), bf16[1024,576]{0,1:T(8,128)(2,1)}) %all-gather.3.cloned.1.call-update) | async-done | bytes 1179664 | tf_op jit(solution)/shard_map/all_gather | solution.py:25
  97.1 2.3 %fusion.36 = (bf16[1024,288]{0,1:T(8,128)(2,1)}, bf16[1024,288]{0,1:T(8,128)(2,1)}) fusion(bf16[1024,576]{0,1:T(8,128)(2,1)} %all-gather.3.cloned.1.call-done), kind=kLoop, calls=%fused_computation.62 | loop fusion | bytes 2359296 | tf_op jit(solution)/shard_map/slice | solution.py:26
  99.4 2.2 %reshape.94 = bf16[2,512,4,72]{1,0,3,2:T(2,128)(2,1)S(1)} reshape(bf16[1024,288]{0,1:T(8,128)(2,1)} %get-tuple-element.99) | data formatting | bytes 1179648 | tf_op jit(solution)/shard_map/reshape | solution.py:29
  101.6 0.9 copy.30
  102.5 2.4 %reshape.96 = bf16[2,512,4,72]{1,0,3,2:T(2,128)(2,1)S(1)} reshape(bf16[1024,288]{0,1:T(8,128)(2,1)} %get-tuple-element.98) | data formatting | bytes 1179648 | tf_op jit(solution)/shard_map/reshape | solution.py:30
  104.9 0.9 copy.31
  105.8 28.8 %reduce-scatter.2.cloned.1.call-done = bf16[320,1152]{1,0:T(8,128)(2,1)} async-done(((bf16[1280,1152]{1,0:T(8,128)(2,1)}), bf16[320,1152]{1,0:T(8,128)(2,1)}) %reduce-scatter.2.cloned.1.call-update) | async-done | bytes 737296 | tf_op jit(solution)/shard_map/reduce_scatter | solution.py:86
  134.6 2.1 %add_convert_fusion = bf16[320,1152]{1,0:T(8,128)(2,1)} fusion(bf16[320,1152]{1,0:T(8,128)(2,1)} %reduce-scatter.2.cloned.1.call-done, f32[1152]{0:T(1024)S(1)} %reduce.1), kind=kLoop, calls=%fused_computation.36 | loop fusion | flops 1105920 | bytes 1479168 | tf_op jit(solution)/shard_map/convert_element_type | solution.py:92
  136.7 4.6 %all-to-all-start.1 = ((bf16[4,80,1152]{2,1,0:T(8,128)(2,1)}), bf16[4,80,1152]{2,1,0:T(8,128)(2,1)S(1)}, u32[]{:S(2)}, u32[]{:S(2)}) async-start(bf16[4,80,1152]{2,1,0:T(8,128)(2,1)} %bitcast.78), calls=%async_computation.2 | async-start | bytes 1474560 | tf_op jit(solution)/shard_map/all_to_all | solution.py:93
  141.3 14.4 %while.15 = (s32[]{:T(128)}, f32[4,256]{1,0:T(4,128)S(1)}, f32[4,256]{1,0:T(4,128)S(1)}, f32[4,256,72]{1,2,0:T(8,128)}, bf16[2,512,4,72]{1,3,2,0:T(8,128)(2,1)},...) while((s32[]{:T(128)}, f32[4,256]{1,0:T(4,128)S(1)}, ...), condition=%wide.region_3.4_spmd.clone, body=%wide.region_0.3_spmd.clone.sunk | while | flops 155415552 | bytes 16073861 | solution.py:51
  141.3 2.8 %bitcast_reduce_fusion.2 = (f32[4,256]{1,0:T(4,128)S(1)}, f32[4,512,256]{2,1,0:T(8,128)}) fusion(bf16[256,4,72]{0,2,1:T(8,128)(2,1)S(1)} %get-tuple-element.178, bf16[2,512,4,72]{1,3,2,0:T(8,128)(2,1)} %get-tuple-element.177, s32[]{:T(128)} %get-tuple-element.164), kind=kOutput, calls=%fused_computation.2.clone.1 | convolution fusion | flops 76545024 | bytes 2544128 | tf_op jit(solution)/shard_map/while/body/eval_jaxpr/qhd,khd->hqk/dot_general | solution.py:36
  144.1 2.1 %fusion.48 = f32[4,256]{1,0:T(4,128)S(1)} fusion(f32[4,512,256]{2,1,0:T(8,128)} %get-tuple-element.152, f32[4,256]{1,0:T(4,128)S(1)} %select_maximum_fusion.2), kind=kLoop, calls=%fused_computation.5.clone.1 | loop fusion | flops 1571840 | bytes 2105344 | tf_op jit(solution)/shard_map/while/body/eval_jaxpr/reduce_sum | solution.py:42
  146.3 2.1 %convolution_add_fusion.3 = f32[4,256,72]{1,2,0:T(8,128)} fusion(f32[4,512,256]{2,1,0:T(8,128)S(1)} %copy-done.1, f32[4,256]{1,0:T(4,128)S(1)} %select_maximum_fusion.2, f32[4,256,72]{1,2,0:T(8,128)} %get-tuple-element.167, bf16[2,512,4,72]{1,3,2,0:T(8,128)(2,1)} %get-tuple-element.179, s32[]{:T(128)} %get-tuple-element.164, ...), kind=kOutput, calls=%fused_computation.6.clone.1 | convolution fusion | flops 77291520 | bytes 2990593 | tf_op jit(solution)/shard_map/while/body/eval_jaxpr/hqk,khd->hqd/dot_general | solution.py:43
  148.5 2.8 %bitcast_reduce_fusion.2 = (f32[4,256]{1,0:T(4,128)S(1)}, f32[4,512,256]{2,1,0:T(8,128)}) fusion(bf16[256,4,72]{0,2,1:T(8,128)(2,1)S(1)} %get-tuple-element.178, bf16[2,512,4,72]{1,3,2,0:T(8,128)(2,1)} %get-tuple-element.177, s32[]{:T(128)} %get-tuple-element.164), kind=kOutput, calls=%fused_computation.2.clone.1 | convolution fusion | flops 76545024 | bytes 2544128 | tf_op jit(solution)/shard_map/while/body/eval_jaxpr/qhd,khd->hqk/dot_general | solution.py:36
  151.3 2.1 %fusion.48 = f32[4,256]{1,0:T(4,128)S(1)} fusion(f32[4,512,256]{2,1,0:T(8,128)} %get-tuple-element.152, f32[4,256]{1,0:T(4,128)S(1)} %select_maximum_fusion.2), kind=kLoop, calls=%fused_computation.5.clone.1 | loop fusion | flops 1571840 | bytes 2105344 | tf_op jit(solution)/shard_map/while/body/eval_jaxpr/reduce_sum | solution.py:42
  153.5 2.2 %convolution_add_fusion.3 = f32[4,256,72]{1,2,0:T(8,128)} fusion(f32[4,512,256]{2,1,0:T(8,128)S(1)} %copy-done.1, f32[4,256]{1,0:T(4,128)S(1)} %select_maximum_fusion.2, f32[4,256,72]{1,2,0:T(8,128)} %get-tuple-element.167, bf16[2,512,4,72]{1,3,2,0:T(8,128)(2,1)} %get-tuple-element.179, s32[]{:T(128)} %get-tuple-element.164, ...), kind=kOutput, calls=%fused_computation.6.clone.1 | convolution fusion | flops 77291520 | bytes 2990593 | tf_op jit(solution)/shard_map/while/body/eval_jaxpr/hqk,khd->hqd/dot_general | solution.py:43
  155.8 1.6 divide_convert_fusion
  157.4 2.8 %all-to-all-done.1 = bf16[4,80,1152]{2,1,0:T(8,128)(2,1)S(1)} async-done(((bf16[4,80,1152]{2,1,0:T(8,128)(2,1)}), bf16[4,80,1152]{2,1,0:T(8,128)(2,1)S(1)}, u32[]{:S(2)}, u32[]{:S(2)}) %all-to-all-start.1) | async-done | bytes 737312 | tf_op jit(solution)/shard_map/all_to_all | solution.py:93
  160.2 2.1 %gather_fusion = bf16[256,1152]{1,0:T(8,128)(2,1)} fusion(bf16[320,1152]{1,0:T(8,128)(2,1)S(1)} %bitcast.76, s32[1024]{0:T(1024)S(1)} %pad_clamp_fusion), kind=kCustom, calls=%fused_computation | custom fusion | bytes 1180672 | tf_op jit(solution)/shard_map/gather | solution.py:95
  162.3 2.8 %reshape.102 = f32[128,2,1152]{2,1,0:T(2,128)} reshape(bf16[256,1152]{1,0:T(8,128)(2,1)} %gather_fusion) | data formatting | bytes 1769472 | tf_op jit(solution)/shard_map/convert_element_type | solution.py:95
  165.1 3.5 %multiply_reduce_fusion = bf16[128,1152]{1,0:T(8,128)(2,1)} fusion(f32[128,2,1152]{2,1,0:T(2,128)} %reshape.102, f32[128,2]{1,0:T(8,128)S(1)} %copy-done.3), kind=kLoop, calls=%fused_computation.37 | loop fusion | flops 442368 | bytes 1475584 | tf_op jit(solution)/shard_map/reduce_sum | solution.py:96
  (60 shorter events, 1.4 us)
Async XLA Ops:
  7.2 56.6 %copy-start = (bf16[1,1152,1152]{2,1,0:T(8,128)(2,1)S(1)}, bf16[1,1152,1152]{2,1,0:T(8,128)(2,1)}, u32[]{:S(2)}) copy-start(bf16[1,1152,1152]{2,1,0:T(8,128)(2,1)} %param.26) | copy-start | bytes 7962628
  7.2 30.0 %copy-start.11 = (s32[2]{0:T(128)S(1)}, s32[2]{0:T(128)}, u32[]{:S(2)}) copy-start(s32[2]{0:T(128)} %param.20) | copy-start | bytes 28
  7.2 30.0 %copy-start.4 = (bf16[256,288]{0,1:T(8,128)(2,1)S(1)}, bf16[256,288]{0,1:T(8,128)(2,1)}, u32[]{:S(2)}) copy-start(bf16[256,288]{0,1:T(8,128)(2,1)} %param.16) | copy-start | bytes 442372
  7.2 30.0 %copy-start.6 = (bf16[256,288]{0,1:T(8,128)(2,1)S(1)}, bf16[256,288]{0,1:T(8,128)(2,1)}, u32[]{:S(2)}) copy-start(bf16[256,288]{0,1:T(8,128)(2,1)} %param.17) | copy-start | bytes 442372
  7.2 30.0 %copy-start.5 = (bf16[256,288]{0,1:T(8,128)(2,1)S(1)}, bf16[256,288]{0,1:T(8,128)(2,1)}, u32[]{:S(2)}) copy-start(bf16[256,288]{0,1:T(8,128)(2,1)} %param.18) | copy-start | bytes 442372
  7.2 30.0 %copy-start.7 = (bf16[256,288]{0,1:T(8,128)(2,1)S(1)}, bf16[256,288]{0,1:T(8,128)(2,1)}, u32[]{:S(2)}) copy-start(bf16[256,288]{0,1:T(8,128)(2,1)} %param.19) | copy-start | bytes 442372
  7.2 56.5 %all-gather.5.cloned.1.call-start = ((), (), s32[]{:S(2)}) async-start(), calls=%async_computation.4 | async-start | bytes 3686400 | tf_op jit(solution)/shard_map/all_gather | solution.py:82
  10.4 27.8 %copy-start.8 = (f32[1,1152]{1,0:T(1,128)S(1)}, f32[1,1152]{1,0:T(1,128)}, u32[]{:S(2)}) copy-start(f32[1,1152]{1,0:T(1,128)} %param.25) | copy-start | bytes 13828
  37.1 60.0 %all-gather.3.cloned.1.call-start = ((), (), s32[]{:S(2)}) async-start(), calls=%async_computation.3 | async-start | bytes 1474560 | tf_op jit(solution)/shard_map/all_gather | solution.py:25
  38.1 96.5 %reduce-scatter.2.cloned.1.call-start = ((), (), s32[]{:S(2)}) async-start(), calls=%async_computation.5 | async-start | bytes 3686400 | tf_op jit(solution)/shard_map/reduce_scatter | solution.py:86
  76.0 0.7 copy-start.9
  76.0 0.7 copy-start.10
  102.5 38.8 %copy-start.2 = (bf16[256,288]{0,1:T(8,128)(2,1)S(1)}, bf16[256,288]{0,1:T(8,128)(2,1)}, u32[]{:S(2)}) copy-start(bf16[256,288]{0,1:T(8,128)(2,1)} %param.15) | copy-start | bytes 442372
  136.7 23.5 %all-to-all-start.1 = ((bf16[4,80,1152]{2,1,0:T(8,128)(2,1)}), bf16[4,80,1152]{2,1,0:T(8,128)(2,1)S(1)}, u32[]{:S(2)}, u32[]{:S(2)}) async-start(bf16[4,80,1152]{2,1,0:T(8,128)(2,1)} %bitcast.78), calls=%async_computation.2 | async-start | bytes 1474560 | tf_op jit(solution)/shard_map/all_to_all | solution.py:93
  144.1 2.2 %copy-start.1 = (f32[4,512,256]{2,1,0:T(8,128)S(1)}, f32[4,512,256]{2,1,0:T(8,128)}, u32[]{:S(2)}) copy-start(f32[4,512,256]{2,1,0:T(8,128)} %get-tuple-element.152) | copy-start | bytes 6291460 | tf_op jit(solution)/shard_map/while
  151.3 2.2 %copy-start.1 = (f32[4,512,256]{2,1,0:T(8,128)S(1)}, f32[4,512,256]{2,1,0:T(8,128)}, u32[]{:S(2)}) copy-start(f32[4,512,256]{2,1,0:T(8,128)} %get-tuple-element.152) | copy-start | bytes 6291460 | tf_op jit(solution)/shard_map/while
  160.2 4.9 %copy-start.3 = (f32[128,2]{1,0:T(8,128)S(1)}, f32[128,2]{1,0:T(8,128)}, u32[]{:S(2)}) copy-start(f32[128,2]{1,0:T(8,128)} %copy.38) | copy-start | bytes 3076
Sparse Core Ops, SparseCore 0:
  37.2 26.4 all-gather.4
  65.3 31.7 all-gather.2
  99.6 34.9 reduce-scatter.1

commit v2 on v1

v2 whole, which is shorter than its diff:
```python
import functools
import math

import jax
import jax.numpy as jnp
from jax import lax
from jax.experimental import pallas as pl
from jax.experimental.pallas import tpu as pltpu
from jax.sharding import PartitionSpec as P

HD = 72
MESH = pl.DeviceIdType.MESH
F32 = jnp.float32
BF16 = jnp.bfloat16


def layer_kernel(
    sizes,
    q_ref, fresh_k, fresh_v, stale_k, stale_v, flags,
    tok_ref, ids_ref, idst_ref, gate_ref,
    up_hbm, upb_ref, down_hbm, downb_ref,
    attn_ref, moe_ref,
    up_v, down_v, place_v, disp, rows, tpin, xin, fin, ret, kv, acc,
    w_sem,
    z_send, z_recv, xf_send, xf_recv, tf_send, tf_recv,
    tr_send, tr_recv, xr_send, xr_recv, zr_send, zr_recv, kv_send, kv_recv,
):
    S, X, capp = sizes
    s, x, c = lax.axis_index("seq"), lax.axis_index("exp"), lax.axis_index("tp")
    oc = 1 - c
    T, D = tok_ref.shape
    L, W = q_ref.shape
    heads = W // HD
    blk = L // flags.shape[0]

    up_copy = pltpu.make_async_copy(up_hbm.at[0], up_v, w_sem.at[0])
    down_copy = pltpu.make_async_copy(down_hbm.at[0], down_v, w_sem.at[1])
    up_copy.start()
    down_copy.start()

    def rdma(src, dst, ssem, rsem, where):
        return pltpu.make_async_remote_copy(
            src_ref=src, dst_ref=dst, send_sem=ssem, recv_sem=rsem,
            device_id=where, device_id_type=MESH,
        )

    def z_copy(e, slot):
        return rdma(disp.at[e], rows.at[slot, c, x], z_send.at[e], z_recv.at[slot], {"seq": e})

    def x_forward(src, to, origin):
        return rdma(
            rows.at[src, c, origin], rows.at[src, c, origin],
            xf_send.at[src, to], xf_recv.at[src, origin], {"exp": to},
        )

    def t_forward(src, origin, side):
        return rdma(
            rows.at[src, side, origin], rows.at[src, side, origin],
            tf_send.at[src, origin], tf_recv.at[src, origin], {"tp": oc},
        )

    def t_reduce(src):
        return rdma(rows.at[src, oc], tpin.at[src], tr_send.at[src], tr_recv.at[src], {"tp": oc})

    def x_reduce(src, to, origin):
        return rdma(
            rows.at[src, c, to], xin.at[src, origin],
            xr_send.at[src, to], xr_recv.at[src, origin], {"exp": to},
        )

    def z_return(src, slot):
        return rdma(fin.at[src], ret.at[slot], zr_send.at[src], zr_recv.at[slot], {"seq": src})

    def kv_copy(to, slot):
        return rdma(kv.at[slot], kv.at[slot], kv_send.at[to], kv_recv.at[slot], {"seq": to})

    def other_x(i):
        return lax.rem(x + i, X)

    def order(k):
        half = (k + 1) // 2
        return lax.rem(s + half * (2 * lax.rem(k, 2) - 1) + S, S)

    barrier = pltpu.get_barrier_semaphore()
    for i in range(1, S):
        pl.semaphore_signal(barrier, inc=1, device_id={"seq": lax.rem(s + i, S)}, device_id_type=MESH)
    for i in range(1, X):
        pl.semaphore_signal(barrier, inc=1, device_id={"exp": other_x(i)}, device_id_type=MESH)
    pl.semaphore_signal(barrier, inc=1, device_id={"tp": oc}, device_id_type=MESH)

    expert = lax.broadcasted_iota(jnp.int32, (S, T), 0)
    named = (idst_ref[0:1, :] == expert) | (idst_ref[1:2, :] == expert)
    earlier = lax.broadcasted_iota(jnp.int32, (T, T), 0) < lax.broadcasted_iota(jnp.int32, (T, T), 1)
    place = jnp.dot(
        jnp.where(named, 1.0, 0.0).astype(BF16),
        jnp.where(earlier, 1.0, 0.0).astype(BF16),
        preferred_element_type=F32,
    )
    place_v[...] = jnp.where(named, place, -1.0)
    slot_rows = lax.broadcasted_iota(jnp.int32, (capp, T), 0).astype(F32)

    def slots_of(e):
        pick = jnp.where(place_v[pl.ds(e, 1), :] == slot_rows, 1.0, 0.0).astype(BF16)
        return jnp.dot(pick, tok_ref[...], preferred_element_type=F32).astype(BF16)

    def forward(src):
        for i in range(1, X):
            x_forward(src, other_x(i), x).start()
        t_forward(src, x, c).start()

    rows[s, c, x] = slots_of(s)
    pl.semaphore_wait(barrier, S - 1 + X - 1 + 1)
    forward(s)
    for k in range(1, S):
        e = order(k)
        disp[e] = slots_of(e)
        z_copy(e, s).start()

    for b in range(flags.shape[0]):
        fresh = flags[b] == 1
        part = pl.ds(b * blk, blk)
        kv[s, 0, part, :] = jnp.where(fresh, fresh_k[part, :], stale_k[part, :])
        kv[s, 1, part, :] = jnp.where(fresh, fresh_v[part, :], stale_v[part, :])
    for k in range(1, S):
        kv_copy(order(k), s).start()

    up_copy.wait()
    down_copy.wait()

    def finish(src):
        total = rows[src, c, x].astype(F32) + downb_ref[...]
        for i in range(1, X):
            x_reduce(src, other_x(i), other_x(i)).wait_recv()
            total = total + xin[src, other_x(i)].astype(F32)
        done = total.astype(BF16)
        fin[src] = done

    def finish_send(src):
        finish(src)

        @pl.when(src != s)
        def _():
            z_return(src, s).start()

        @pl.when(src == s)
        def _():
            ret[s] = fin[s]

    def chunk(k, unused):
        src = order(k)
        for i in range(1, X):
            x_forward(src, other_x(i), other_x(i)).wait_recv()
            t_forward(src, other_x(i), c).start()

        @pl.when(k + 1 < S)
        def _():
            nxt = order(k + 1)
            z_copy(nxt, nxt).wait_recv()
            forward(nxt)

        for i in range(X):
            t_forward(src, other_x(i), oc).wait_recv()
        for i in range(1, X):
            x_forward(src, other_x(i), x).wait_send()
        for i in range(X):
            t_forward(src, other_x(i), c).wait_send()

        block = rows[src].reshape(2 * X * capp, D)
        hidden = jnp.dot(block, up_v[...], preferred_element_type=F32) + upb_ref[...]
        hidden = jax.nn.gelu(hidden).astype(BF16)
        result = jnp.dot(hidden, down_v[...], preferred_element_type=F32).astype(BF16)
        rows[src] = result.reshape(2, X, capp, D)
        t_reduce(src).start()

        @pl.when(k >= 1)
        def _():
            finish_send(order(k - 1))

        t_reduce(src).wait_recv()
        for i in range(X):
            to = other_x(i)
            rows[src, c, to] = (rows[src, c, to].astype(F32) + tpin[src, to].astype(F32)).astype(BF16)
            if i > 0:
                x_reduce(src, to, x).start()
        return unused

    lax.fori_loop(0, S, chunk, jnp.int32(0))

    for i in range(1, S):
        kv_copy(s, lax.rem(s + i, S)).wait_recv()
    scale = 1.0 / math.sqrt(HD)
    column = lax.broadcasted_iota(jnp.int32, (L, W), 1)

    def head(h, unused):
        mine = (column >= h * HD) & (column < (h + 1) * HD)
        query = jnp.where(mine, q_ref[...].astype(F32), 0.0).astype(BF16)
        keys = kv[:, 0].reshape(S * L, W)
        values = kv[:, 1].reshape(S * L, W)
        scores = lax.dot_general(
            query, keys, (((1,), (1,)), ((), ())), preferred_element_type=F32
        ) * scale
        probs = jnp.exp(scores - jnp.max(scores, axis=1, keepdims=True))
        total = jnp.sum(probs, axis=1, keepdims=True)
        mixed = jnp.dot(probs.astype(BF16), values, preferred_element_type=F32) / total
        acc[...] = jnp.where(mine, mixed, acc[...])
        return unused

    acc[...] = jnp.zeros_like(acc)
    first = heads // 2
    if first:
        lax.fori_loop(0, first, head, jnp.int32(0))
    finish_send(order(S - 1))
    lax.fori_loop(first, heads, head, jnp.int32(0))
    attn_ref[...] = acc[...].astype(BF16)

    lane = lax.broadcasted_iota(jnp.int32, (T, S), 1)
    hit0 = ids_ref[:, 0:1] == lane
    hit1 = ids_ref[:, 1:2] == lane
    below = lax.broadcasted_iota(jnp.int32, (T, T), 1) < lax.broadcasted_iota(jnp.int32, (T, T), 0)
    before = jnp.dot(
        jnp.where(below, 1.0, 0.0).astype(BF16),
        jnp.where(hit0 | hit1, 1.0, 0.0).astype(BF16),
        preferred_element_type=F32,
    )
    base = before + (lane * capp).astype(F32)
    slot_lane = lax.broadcasted_iota(jnp.int32, (T, S * capp), 1).astype(F32)
    picks = [
        jnp.where(
            jnp.sum(jnp.where(hit, base, 0.0), axis=1, keepdims=True) == slot_lane, 1.0, 0.0
        ).astype(BF16)
        for hit in (hit0, hit1)
    ]
    for i in range(1, S):
        z_return(s, lax.rem(s + i, S)).wait_recv()
    everything = ret[...].reshape(S * capp, D)
    moe_ref[...] = (
        jnp.dot(picks[0], everything, preferred_element_type=F32) * gate_ref[:, 0:1]
        + jnp.dot(picks[1], everything, preferred_element_type=F32) * gate_ref[:, 1:2]
    ).astype(BF16)

    def drain(i, unused):
        to = lax.rem(s + i, S)
        z_copy(to, s).wait_send()
        kv_copy(to, s).wait_send()
        z_return(to, s).wait_send()
        return unused

    lax.fori_loop(1, S, drain, jnp.int32(0))

    def drain_chunk(i, unused):
        t_reduce(i).wait_send()
        for j in range(1, X):
            x_reduce(i, other_x(j), x).wait_send()
        return unused

    lax.fori_loop(0, S, drain_chunk, jnp.int32(0))


def local(
    attn_query, fresh_keys, fresh_values, stale_keys, stale_values, block_flags,
    moe_tokens, expert_ids, gate_weights, up_weight, up_bias, down_weight, down_bias,
):
    S, X = lax.axis_size("seq"), lax.axis_size("exp")
    assert lax.axis_size("tp") == 2 and up_weight.shape[0] == 1
    tokens, D = moe_tokens.shape
    length, width = attn_query.shape
    hidden = up_weight.shape[2]
    cap = 5 * tokens // (2 * S)
    capp = -(-cap // 16) * 16
    vmem = pl.BlockSpec(memory_space=pltpu.VMEM)
    smem = pl.BlockSpec(memory_space=pltpu.SMEM)
    hbm = pl.BlockSpec(memory_space=pl.ANY)
    dma = pltpu.SemaphoreType.DMA
    return pl.pallas_call(
        functools.partial(layer_kernel, (S, X, capp)),
        out_shape=(
            jax.ShapeDtypeStruct((length, width), BF16),
            jax.ShapeDtypeStruct((tokens, D), BF16),
        ),
        in_specs=[vmem] * 5 + [smem] + [vmem] * 4 + [hbm, vmem, hbm, vmem],
        out_specs=(vmem, vmem),
        scratch_shapes=[
            pltpu.VMEM((D, hidden), BF16),
            pltpu.VMEM((hidden, D), BF16),
            pltpu.VMEM((S, tokens), F32),
            pltpu.VMEM((S, capp, D), BF16),
            pltpu.VMEM((S, 2, X, capp, D), BF16),
            pltpu.VMEM((S, X, capp, D), BF16),
            pltpu.VMEM((S, X, capp, D), BF16),
            pltpu.VMEM((S, capp, D), BF16),
            pltpu.VMEM((S, capp, D), BF16),
            pltpu.VMEM((S, 2, length, width), BF16),
            pltpu.VMEM((length, width), F32),
            dma((2,)),
            dma((S,)), dma((S,)), dma((S, X)), dma((S, X)), dma((S, X)), dma((S, X)),
            dma((S,)), dma((S,)), dma((S, X)), dma((S, X)), dma((S,)), dma((S,)),
            dma((S,)), dma((S,)),
        ],
        compiler_params=pltpu.CompilerParams(
            collective_id=0, has_side_effects=True, vmem_limit_bytes=67043328
        ),
    )(
        attn_query, fresh_keys, fresh_values, stale_keys, stale_values, block_flags,
        moe_tokens, expert_ids, expert_ids.T, gate_weights,
        up_weight, up_bias, down_weight, down_bias,
    )


def solution(mesh):
    in_specs = (
        P(("groups", "seq"), ("exp", "tp")),
        P(("groups", "seq"), ("exp", "tp")),
        P(("groups", "seq"), ("exp", "tp")),
        P(("groups", "seq"), ("exp", "tp")),
        P(("groups", "seq"), ("exp", "tp")),
        P(("groups", "seq")),
        P(("groups", "seq", "exp", "tp"), None),
        P(("groups", "seq", "exp", "tp"), None),
        P(("groups", "seq", "exp", "tp"), None),
        P("seq", None, ("exp", "tp")),
        P("seq", ("exp", "tp")),
        P("seq", ("exp", "tp"), None),
        P("seq", None),
    )
    out_specs = (P(("groups", "seq"), ("exp", "tp")), P(("groups", "seq", "exp", "tp"), None))
    return jax.shard_map(local, mesh=mesh, in_specs=in_specs, out_specs=out_specs, check_vma=False)
```

time: 176 us -> 91.2 us (0.52)
  waiting for transfers between devices: 76.8 us -> 0 us
  Pallas kernels: 0 us -> 75.4 us
  blocking collectives: 25.3 us -> 0 us
  matrix products: 23.6 us -> 0 us
  other arithmetic: 13.8 us -> 0 us
  between operations: 14 us -> 0.64 us
  starting transfers between devices: 4.73 us -> 0 us
  local copies, waits for them, and re-layouts: 16.9 us -> 14.8 us
    pallas_call x0 -> x1, Pallas kernels: none -> 75.4 us  [local(): pl.pallas_call(functools.partial(layer_kernel, (S, X, capp)), out_shape=(...]
    all_gather x2 -> x0, waiting for transfers between devices: 45.1 us -> none  [the longest x1 25.6 us: expert_part(): chip_rows = lax.all_gather(flat_rows, ('exp', 'tp'), axis=0, tiled=True)]
    reduce_scatter x1 -> x0, waiting for transfers between devices: 28.8 us -> none  [expert_part(): lax.psum_scatter(jnp.dot(hidden, down_weight[0], preferred_element_type=j...]
    all_to_all x1 -> x0, blocking collectives: 25.3 us -> none  [expert_part(): lax.all_to_all(buffer, 'seq', split_axis=0, concat_axis=0, tiled=True)]
    dot_general x6 -> x0, matrix products: 23.6 us -> none  [the longest x1 12.3 us: expert_part(): jnp.dot(hidden, down_weight[0], preferred_element_type=jnp.float32)]
    unnamed x26 -> x8, local copies, waits for them, and re-layouts: 3.97 us -> 13.1 us
    reduce_sum x5 -> x0, other arithmetic: 7.78 us -> none  [the longest x2 4.2 us: advance(): totals = totals * rescale + jnp.sum(probs, axis=-1)]
    all_to_all x1 -> x0, starting transfers between devices: 4.61 us -> none  [expert_part(): lax.all_to_all(result, 'seq', split_axis=0, concat_axis=0, tiled=True)]
  transfers between devices with their start and end apart: 4 -> 0, of which waited for: 4 -> 0; matrix products, arithmetic and copies ran while one was open for 22% -> 0% of each run, Pallas kernels for 0% -> 0%
where the time goes in v2:
time: 91.2 us; the launch traced here: 90.9 us
  Pallas kernels  75.4 us (83%)
  local copies, waits for them, and re-layouts  14.8 us (16%)
    pallas_call x1, Pallas kernels, local(): pl.pallas_call(functools.partial(layer_kernel, (S, X, capp)), out_shape=(...  75.4 us
    unnamed x8, local copies, waits for them, and re-layouts  13.1 us

profile of v2, /device:TPU:0, one launch (start us, length us, event | category | flops | bytes accessed | tf_op | source)
XLA Modules:
  0.0 90.9 jit_solution(14812326807284960085)
XLA Ops:
  0.6 1.4 %copy.21.gate_ref = f32[128,2]{1,0:T(8,128)} copy(f32[128,2]{0,1:T(2,128)} %param.21) | data formatting | bytes 2048 | tf_op args[8]
  2.0 1.4 %copy.20.ids_ref = s32[128,2]{1,0:T(8,128)} copy(s32[128,2]{0,1:T(2,128)} %param.20) | data formatting | bytes 2048 | tf_op args[7]
  3.4 1.7 %copy.15.q_ref = bf16[256,288]{1,0:T(8,128)(2,1)} copy(bf16[256,288]{0,1:T(8,128)(2,1)} %param.13) | data formatting | bytes 294912 | tf_op args[0]
  5.2 1.7 %copy.16.fresh_k = bf16[256,288]{1,0:T(8,128)(2,1)} copy(bf16[256,288]{0,1:T(8,128)(2,1)} %param.14) | data formatting | bytes 294912 | tf_op args[1]
  6.9 1.7 %copy.17.fresh_v = bf16[256,288]{1,0:T(8,128)(2,1)} copy(bf16[256,288]{0,1:T(8,128)(2,1)} %param.15) | data formatting | bytes 294912 | tf_op args[2]
  8.6 1.7 %copy.18.stale_k = bf16[256,288]{1,0:T(8,128)(2,1)} copy(bf16[256,288]{0,1:T(8,128)(2,1)} %param.16) | data formatting | bytes 294912 | tf_op args[3]
  10.4 1.7 %copy.19.stale_v = bf16[256,288]{1,0:T(8,128)(2,1)} copy(bf16[256,288]{0,1:T(8,128)(2,1)} %param.17) | data formatting | bytes 294912 | tf_op args[4]
  12.1 75.4 %shard_map.140 = (bf16[256,288]{1,0:T(8,128)(2,1)}, bf16[128,1152]{1,0:T(8,128)(2,1)}) custom-call(bf16[256,288]{1,0:T(8,128)(2,1)} %copy.15.q_ref, bf16[256,288]{1,0:T(8,128)(2,1)} %copy.16.fresh_k, bf16[256,288]{1,0:T(8,128)(2,1)} %copy.17.fresh_v, bf16[256,288]{1,0:T(8,128)(2,1)} %copy.18.stale_k, bf16[256,288]{1,0:T(8,128)(2,1)} %copy.19.stale_v, ...), custom_call_target="tpu_custom_call" | custom-call | tf_op jit(solution)/shard_map/pallas_call | solution.py:274
  87.5 1.7 %copy.22 = bf16[256,288]{0,1:T(8,128)(2,1)} copy(bf16[256,288]{1,0:T(8,128)(2,1)} %get-tuple-element.2) | data formatting | bytes 294912 | tf_op jit(solution)/shard_map/pallas_call | solution.py:274
  89.2 1.7 %copy.24 = bf16[128,1152]{1,0:T(8,128)(2,1)} copy(bf16[128,1152]{1,0:T(8,128)(2,1)} %get-tuple-element.7) | data formatting | bytes 589824

commit v3 on v2

--- a/solution.py
+++ b/solution.py
@@ -17,19 +17,19 @@
 def layer_kernel(
     sizes,
     q_ref, fresh_k, fresh_v, stale_k, stale_v, flags,
-    tok_ref, ids_ref, idst_ref, gate_ref,
+    tok_ref, ids_ref, gate_ref,
     up_hbm, upb_ref, down_hbm, downb_ref,
     attn_ref, moe_ref,
-    up_v, down_v, place_v, disp, rows, tpin, xin, fin, ret, kv, acc,
+    up_v, down_v, place_v, disp, rows, tpin, xin, fin, ret, kv, keys_v, acc, turn,
     w_sem,
     z_send, z_recv, xf_send, xf_recv, tf_send, tf_recv,
-    tr_send, tr_recv, xr_send, xr_recv, zr_send, zr_recv, kv_send, kv_recv,
+    tr_send, tr_recv, xr_send, xr_recv, zr_send, zr_recv, kv_right, kv_left, kv_recv,
 ):
     S, X, capp = sizes
     s, x, c = lax.axis_index("seq"), lax.axis_index("exp"), lax.axis_index("tp")
     oc = 1 - c
     T, D = tok_ref.shape
-    L, W = q_ref.shape
+    W, L = q_ref.shape
     heads = W // HD
     blk = L // flags.shape[0]
 
@@ -71,13 +71,15 @@
     def z_return(src, slot):
         return rdma(fin.at[src], ret.at[slot], zr_send.at[src], zr_recv.at[slot], {"seq": src})
 
-    def kv_copy(to, slot):
-        return rdma(kv.at[slot], kv.at[slot], kv_send.at[to], kv_recv.at[slot], {"seq": to})
+    def kv_copy(b, step):
+        sems = kv_right if step > 0 else kv_left
+        return rdma(kv.at[b], kv.at[b], sems.at[b], kv_recv.at[b], {"seq": s + step})
 
     def other_x(i):
         return lax.rem(x + i, X)
 
     def order(k):
+        k = lax.rem(k + 1, S)
         half = (k + 1) // 2
         return lax.rem(s + half * (2 * lax.rem(k, 2) - 1) + S, S)
 
@@ -89,7 +91,7 @@
     pl.semaphore_signal(barrier, inc=1, device_id={"tp": oc}, device_id_type=MESH)
 
     expert = lax.broadcasted_iota(jnp.int32, (S, T), 0)
-    named = (idst_ref[0:1, :] == expert) | (idst_ref[1:2, :] == expert)
+    named = (ids_ref[0:1, :] == expert) | (ids_ref[1:2, :] == expert)
     earlier = lax.broadcasted_iota(jnp.int32, (T, T), 0) < lax.broadcasted_iota(jnp.int32, (T, T), 1)
     place = jnp.dot(
         jnp.where(named, 1.0, 0.0).astype(BF16),
@@ -111,7 +113,7 @@
     rows[s, c, x] = slots_of(s)
     pl.semaphore_wait(barrier, S - 1 + X - 1 + 1)
     forward(s)
-    for k in range(1, S):
+    for k in range(S - 1):
         e = order(k)
         disp[e] = slots_of(e)
         z_copy(e, s).start()
@@ -119,10 +121,35 @@
     for b in range(flags.shape[0]):
         fresh = flags[b] == 1
         part = pl.ds(b * blk, blk)
-        kv[s, 0, part, :] = jnp.where(fresh, fresh_k[part, :], stale_k[part, :])
-        kv[s, 1, part, :] = jnp.where(fresh, fresh_v[part, :], stale_v[part, :])
-    for k in range(1, S):
-        kv_copy(order(k), s).start()
+        kv[s, 0, :, part] = jnp.where(fresh, fresh_k[:, part], stale_k[:, part])
+        kv[s, 1, :, part] = jnp.where(fresh, fresh_v[:, part], stale_v[:, part])
+
+    def relay(step):
+        low, high = s - (step - 1), s + (step - 1)
+
+        @pl.when(low >= 0)
+        def _():
+            @pl.when(low < s)
+            def _():
+                kv_copy(low, 1).wait_recv()
+
+            @pl.when(s + 1 < S)
+            def _():
+                kv_copy(low, 1).start()
+
+        @pl.when(high < S)
+        def _():
+            @pl.when(high > s)
+            def _():
+                kv_copy(high, -1).wait_recv()
+
+            @pl.when(s - 1 >= 0)
+            def _():
+                kv_copy(high, -1).start()
+
+    relay(jnp.int32(1))
+    z_copy(order(0), order(0)).wait_recv()
+    forward(order(0))
 
     up_copy.wait()
     down_copy.wait()
@@ -152,7 +179,7 @@
             x_forward(src, other_x(i), other_x(i)).wait_recv()
             t_forward(src, other_x(i), c).start()
 
-        @pl.when(k + 1 < S)
+        @pl.when(k + 1 < S - 1)
         def _():
             nxt = order(k + 1)
             z_copy(nxt, nxt).wait_recv()
@@ -175,6 +202,7 @@
         @pl.when(k >= 1)
         def _():
             finish_send(order(k - 1))
+            relay(k + 1)
 
         t_reduce(src).wait_recv()
         for i in range(X):
@@ -186,62 +214,49 @@
 
     lax.fori_loop(0, S, chunk, jnp.int32(0))
 
-    for i in range(1, S):
-        kv_copy(s, lax.rem(s + i, S)).wait_recv()
+    for i in range(S):
+        keys_v[pl.ds(i * L, L), :] = kv[i, 0].T
     scale = 1.0 / math.sqrt(HD)
-    column = lax.broadcasted_iota(jnp.int32, (L, W), 1)
+    channel = lax.broadcasted_iota(jnp.int32, (W, L), 0)
 
     def head(h, unused):
-        mine = (column >= h * HD) & (column < (h + 1) * HD)
+        mine = (channel >= h * HD) & (channel < (h + 1) * HD)
         query = jnp.where(mine, q_ref[...].astype(F32), 0.0).astype(BF16)
-        keys = kv[:, 0].reshape(S * L, W)
-        values = kv[:, 1].reshape(S * L, W)
-        scores = lax.dot_general(
-            query, keys, (((1,), (1,)), ((), ())), preferred_element_type=F32
-        ) * scale
-        probs = jnp.exp(scores - jnp.max(scores, axis=1, keepdims=True))
-        total = jnp.sum(probs, axis=1, keepdims=True)
-        mixed = jnp.dot(probs.astype(BF16), values, preferred_element_type=F32) / total
-        acc[...] = jnp.where(mine, mixed, acc[...])
+        scores = jnp.dot(keys_v[...], query, preferred_element_type=F32) * scale
+        probs = jnp.exp(scores - jnp.max(scores, axis=0, keepdims=True))
+        total = jnp.sum(probs, axis=0, keepdims=True)
+        weights = probs.astype(BF16)
+        mixed = jnp.zeros((W, L), F32)
+        for i in range(S):
+            mixed += jnp.dot(kv[i, 1], weights[i * L : (i + 1) * L], preferred_element_type=F32)
+        acc[...] = jnp.where(mine, mixed / total, acc[...])
         return unused
 
     acc[...] = jnp.zeros_like(acc)
-    first = heads // 2
-    if first:
-        lax.fori_loop(0, first, head, jnp.int32(0))
+    lax.fori_loop(0, heads, head, jnp.int32(0))
+    attn_ref[...] = acc[...].astype(BF16)
     finish_send(order(S - 1))
-    lax.fori_loop(first, heads, head, jnp.int32(0))
-    attn_ref[...] = acc[...].astype(BF16)
-
-    lane = lax.broadcasted_iota(jnp.int32, (T, S), 1)
-    hit0 = ids_ref[:, 0:1] == lane
-    hit1 = ids_ref[:, 1:2] == lane
-    below = lax.broadcasted_iota(jnp.int32, (T, T), 1) < lax.broadcasted_iota(jnp.int32, (T, T), 0)
-    before = jnp.dot(
-        jnp.where(below, 1.0, 0.0).astype(BF16),
-        jnp.where(hit0 | hit1, 1.0, 0.0).astype(BF16),
-        preferred_element_type=F32,
-    )
-    base = before + (lane * capp).astype(F32)
+
+    base = jnp.where(named, place, 0.0) + (expert * capp).astype(F32)
+    turn[...] = jnp.zeros_like(turn)
+    for j in range(2):
+        hit = ids_ref[j : j + 1, :] == expert
+        turn[j : j + 1, :] = jnp.sum(jnp.where(hit, base, 0.0), axis=0, keepdims=True)
+        turn[2 + j : 3 + j, :] = gate_ref[j : j + 1, :]
+    turned = turn[...].T
     slot_lane = lax.broadcasted_iota(jnp.int32, (T, S * capp), 1).astype(F32)
-    picks = [
-        jnp.where(
-            jnp.sum(jnp.where(hit, base, 0.0), axis=1, keepdims=True) == slot_lane, 1.0, 0.0
-        ).astype(BF16)
-        for hit in (hit0, hit1)
-    ]
+    picks = [jnp.where(turned[:, j : j + 1] == slot_lane, 1.0, 0.0).astype(BF16) for j in range(2)]
     for i in range(1, S):
         z_return(s, lax.rem(s + i, S)).wait_recv()
     everything = ret[...].reshape(S * capp, D)
     moe_ref[...] = (
-        jnp.dot(picks[0], everything, preferred_element_type=F32) * gate_ref[:, 0:1]
-        + jnp.dot(picks[1], everything, preferred_element_type=F32) * gate_ref[:, 1:2]
+        jnp.dot(picks[0], everything, preferred_element_type=F32) * turned[:, 2:3]
+        + jnp.dot(picks[1], everything, preferred_element_type=F32) * turned[:, 3:4]
     ).astype(BF16)
 
     def drain(i, unused):
         to = lax.rem(s + i, S)
         z_copy(to, s).wait_send()
-        kv_copy(to, s).wait_send()
         z_return(to, s).wait_send()
         return unused
 
@@ -251,6 +266,15 @@
         t_reduce(i).wait_send()
         for j in range(1, X):
             x_reduce(i, other_x(j), x).wait_send()
+
+        @pl.when((i <= s) & (s + 1 < S))
+        def _():
+            kv_copy(i, 1).wait_send()
+
+        @pl.when((i >= s) & (s - 1 >= 0))
+        def _():
+            kv_copy(i, -1).wait_send()
+
         return unused
 
     lax.fori_loop(0, S, drain_chunk, jnp.int32(0))
@@ -271,13 +295,13 @@
     smem = pl.BlockSpec(memory_space=pltpu.SMEM)
     hbm = pl.BlockSpec(memory_space=pl.ANY)
     dma = pltpu.SemaphoreType.DMA
-    return pl.pallas_call(
+    attn_out, moe_out = pl.pallas_call(
         functools.partial(layer_kernel, (S, X, capp)),
         out_shape=(
-            jax.ShapeDtypeStruct((length, width), BF16),
+            jax.ShapeDtypeStruct((width, length), BF16),
             jax.ShapeDtypeStruct((tokens, D), BF16),
         ),
-        in_specs=[vmem] * 5 + [smem] + [vmem] * 4 + [hbm, vmem, hbm, vmem],
+        in_specs=[vmem] * 5 + [smem] + [vmem] * 3 + [hbm, vmem, hbm, vmem],
         out_specs=(vmem, vmem),
         scratch_shapes=[
             pltpu.VMEM((D, hidden), BF16),
@@ -289,21 +313,24 @@
             pltpu.VMEM((S, X, capp, D), BF16),
             pltpu.VMEM((S, capp, D), BF16),
             pltpu.VMEM((S, capp, D), BF16),
-            pltpu.VMEM((S, 2, length, width), BF16),
-            pltpu.VMEM((length, width), F32),
+            pltpu.VMEM((S, 2, width, length), BF16),
+            pltpu.VMEM((S * length, width), BF16),
+            pltpu.VMEM((width, length), F32),
+            pltpu.VMEM((128, tokens), F32),
             dma((2,)),
             dma((S,)), dma((S,)), dma((S, X)), dma((S, X)), dma((S, X)), dma((S, X)),
             dma((S,)), dma((S,)), dma((S, X)), dma((S, X)), dma((S,)), dma((S,)),
-            dma((S,)), dma((S,)),
+            dma((S,)), dma((S,)), dma((S,)),
         ],
         compiler_params=pltpu.CompilerParams(
             collective_id=0, has_side_effects=True, vmem_limit_bytes=67043328
         ),
     )(
-        attn_query, fresh_keys, fresh_values, stale_keys, stale_values, block_flags,
-        moe_tokens, expert_ids, expert_ids.T, gate_weights,
+        attn_query.T, fresh_keys.T, fresh_values.T, stale_keys.T, stale_values.T, block_flags,
+        moe_tokens, expert_ids.T, gate_weights.T,
         up_weight, up_bias, down_weight, down_bias,
     )
+    return attn_out.T, moe_out
 
 
 def solution(mesh):

time: 91.2 us -> 68.8 us (0.75)
  local copies, waits for them, and re-layouts: 14.8 us -> 3.28 us
  Pallas kernels: 75.4 us -> 64.7 us
    pallas_call x1, Pallas kernels: 75.4 us -> 64.7 us  [local(): pl.pallas_call(functools.partial(layer_kernel, (S, X, capp)), out_shape=(...]
    unnamed x8 -> x2, local copies, waits for them, and re-layouts: 13.1 us -> 3.28 us
    pallas_call x1 -> x0, local copies, waits for them, and re-layouts: 1.7 us -> none  [local(): pl.pallas_call(functools.partial(layer_kernel, (S, X, capp)), out_shape=(...]
where the time goes in v3:
time: 68.8 us; the launch traced here: 68.6 us
  Pallas kernels  64.7 us (94%)
  local copies, waits for them, and re-layouts  3.28 us (5%)
    pallas_call x1, Pallas kernels, local(): pl.pallas_call(functools.partial(layer_kernel, (S, X, capp)), out_shape=(...  64.7 us
    unnamed x2, local copies, waits for them, and re-layouts  3.28 us

profile of v3, /device:TPU:0, one launch (start us, length us, event | category | flops | bytes accessed | tf_op | source)
XLA Modules:
  0.0 68.6 jit_solution(7550063364024488172)
XLA Ops:
  0.6 64.7 %shard_map.140 = (bf16[288,256]{1,0:T(8,128)(2,1)}, bf16[128,1152]{1,0:T(8,128)(2,1)}) custom-call(bf16[288,256]{1,0:T(8,128)(2,1)} %bitcast.9, bf16[288,256]{1,0:T(8,128)(2,1)} %bitcast.10, bf16[288,256]{1,0:T(8,128)(2,1)} %bitcast.11, bf16[288,256]{1,0:T(8,128)(2,1)} %bitcast.12, bf16[288,256]{1,0:T(8,128)(2,1)} %bitcast.13, s32[2]{0:T(128)} %flags.1, ...), custom_call_target="tpu_custom_call" | custom-call | tf_op jit(solution)/shard_map/pallas_call | solution.py:298
  65.3 1.6 %copy.17 = bf16[256,288]{0,1:T(8,128)(2,1)} copy(bf16[256,288]{0,1:T(8,128)(2,1)} %bitcast.8) | data formatting | bytes 294912
  66.9 1.7 %copy.18 = bf16[128,1152]{1,0:T(8,128)(2,1)} copy(bf16[128,1152]{1,0:T(8,128)(2,1)} %get-tuple-element.9) | data formatting | bytes 589824

commit v4 on v3

--- a/solution.py
+++ b/solution.py
@@ -79,9 +79,13 @@
         return lax.rem(x + i, X)
 
     def order(k):
-        k = lax.rem(k + 1, S)
-        half = (k + 1) // 2
-        return lax.rem(s + half * (2 * lax.rem(k, 2) - 1) + S, S)
+        side = jnp.minimum(s, S - 1 - s)
+        near = k // 2 + 1
+        near = jnp.where(lax.rem(k, 2) == 0, near, -near)
+        far = k - side + 1
+        far = jnp.where(2 * s < S, far, -far)
+        step = jnp.where(k < 2 * side, near, far)
+        return s + jnp.where(k == S - 1, 0, step)
 
     barrier = pltpu.get_barrier_semaphore()
     for i in range(1, S):
@@ -113,11 +117,13 @@
     rows[s, c, x] = slots_of(s)
     pl.semaphore_wait(barrier, S - 1 + X - 1 + 1)
     forward(s)
-    for k in range(S - 1):
-        e = order(k)
+    def dispatch(k):
+        e = order(jnp.int32(k))
         disp[e] = slots_of(e)
         z_copy(e, s).start()
 
+    for k in range(min(2, S - 1)):
+        dispatch(k)
     for b in range(flags.shape[0]):
         fresh = flags[b] == 1
         part = pl.ds(b * blk, blk)
@@ -147,9 +153,12 @@
             def _():
                 kv_copy(high, -1).start()
 
-    relay(jnp.int32(1))
-    z_copy(order(0), order(0)).wait_recv()
-    forward(order(0))
+    relay(1)
+    for k in range(2, S - 1):
+        dispatch(k)
+    nearest = order(jnp.int32(0))
+    z_copy(nearest, nearest).wait_recv()
+    forward(nearest)
 
     up_copy.wait()
     down_copy.wait()
@@ -202,6 +211,13 @@
         @pl.when(k >= 1)
         def _():
             finish_send(order(k - 1))
+
+        @pl.when(k == 0)
+        def _():
+            relay(2)
+
+        @pl.when((k >= 2) & (k < S - 1))
+        def _():
             relay(k + 1)
 
         t_reduce(src).wait_recv()
@@ -213,6 +229,8 @@
         return unused
 
     lax.fori_loop(0, S, chunk, jnp.int32(0))
+
+    relay(S)
 
     for i in range(S):
         keys_v[pl.ds(i * L, L), :] = kv[i, 0].T
@@ -235,7 +253,7 @@
     acc[...] = jnp.zeros_like(acc)
     lax.fori_loop(0, heads, head, jnp.int32(0))
     attn_ref[...] = acc[...].astype(BF16)
-    finish_send(order(S - 1))
+    finish_send(s)
 
     base = jnp.where(named, place, 0.0) + (expert * capp).astype(F32)
     turn[...] = jnp.zeros_like(turn)

time: 68.8 us -> 68.8 us (level)
  no operation moved by 1% of the time
where the time goes in v4:
time: 68.8 us; the launch traced here: 68.6 us
  Pallas kernels  64.6 us (94%)
  local copies, waits for them, and re-layouts  3.28 us (5%)
    pallas_call x1, Pallas kernels, local(): pl.pallas_call(functools.partial(layer_kernel, (S, X, capp)), out_shape=(...  64.6 us
    unnamed x2, local copies, waits for them, and re-layouts  3.28 us

profile of v4, /device:TPU:0, one launch (start us, length us, event | category | flops | bytes accessed | tf_op | source)
XLA Modules:
  0.0 68.6 jit_solution(16999512713926828568)
XLA Ops:
  0.6 64.6 %shard_map.140 = (bf16[288,256]{1,0:T(8,128)(2,1)}, bf16[128,1152]{1,0:T(8,128)(2,1)}) custom-call(bf16[288,256]{1,0:T(8,128)(2,1)} %bitcast.9, bf16[288,256]{1,0:T(8,128)(2,1)} %bitcast.10, bf16[288,256]{1,0:T(8,128)(2,1)} %bitcast.11, bf16[288,256]{1,0:T(8,128)(2,1)} %bitcast.12, bf16[288,256]{1,0:T(8,128)(2,1)} %bitcast.13, s32[2]{0:T(128)} %flags.1, ...), custom_call_target="tpu_custom_call" | custom-call | tf_op jit(solution)/shard_map/pallas_call | solution.py:316
  65.3 1.6 %copy.17 = bf16[256,288]{0,1:T(8,128)(2,1)} copy(bf16[256,288]{0,1:T(8,128)(2,1)} %bitcast.8) | data formatting | bytes 294912
  66.9 1.7 %copy.18 = bf16[128,1152]{1,0:T(8,128)(2,1)} copy(bf16[128,1152]{1,0:T(8,128)(2,1)} %get-tuple-element.9) | data formatting | bytes 589824

commit v5 on v3

--- a/solution.py
+++ b/solution.py
@@ -78,10 +78,18 @@
     def other_x(i):
         return lax.rem(x + i, X)
 
+    side = jnp.minimum(s, S - 1 - s)
+    own_turn = jnp.maximum(1, 2 * side)
+
+    def remote(j):
+        near = j // 2 + 1
+        near = jnp.where(lax.rem(j, 2) == 0, near, -near)
+        far = j - side + 1
+        far = jnp.where(2 * s < S, far, -far)
+        return s + jnp.where(j < 2 * side, near, far)
+
     def order(k):
-        k = lax.rem(k + 1, S)
-        half = (k + 1) // 2
-        return lax.rem(s + half * (2 * lax.rem(k, 2) - 1) + S, S)
+        return jnp.where(k == own_turn, s, remote(jnp.where(k > own_turn, k - 1, k)))
 
     barrier = pltpu.get_barrier_semaphore()
     for i in range(1, S):
@@ -113,8 +121,8 @@
     rows[s, c, x] = slots_of(s)
     pl.semaphore_wait(barrier, S - 1 + X - 1 + 1)
     forward(s)
-    for k in range(S - 1):
-        e = order(k)
+    for j in range(S - 1):
+        e = remote(jnp.int32(j))
         disp[e] = slots_of(e)
         z_copy(e, s).start()
 
@@ -147,9 +155,10 @@
             def _():
                 kv_copy(high, -1).start()
 
-    relay(jnp.int32(1))
-    z_copy(order(0), order(0)).wait_recv()
-    forward(order(0))
+    relay(1)
+    nearest = order(jnp.int32(0))
+    z_copy(nearest, nearest).wait_recv()
+    forward(nearest)
 
     up_copy.wait()
     down_copy.wait()
@@ -179,9 +188,11 @@
             x_forward(src, other_x(i), other_x(i)).wait_recv()
             t_forward(src, other_x(i), c).start()
 
-        @pl.when(k + 1 < S - 1)
-        def _():
-            nxt = order(k + 1)
+        nxt = order(k + 1)
+        late = (k == own_turn) & (k == 1)
+
+        @pl.when((k + 1 < S) & (nxt != s) & jnp.logical_not(late))
+        def _():
             z_copy(nxt, nxt).wait_recv()
             forward(nxt)
 
@@ -202,6 +213,14 @@
         @pl.when(k >= 1)
         def _():
             finish_send(order(k - 1))
+
+        @pl.when((k + 1 < S) & late)
+        def _():
+            z_copy(nxt, nxt).wait_recv()
+            forward(nxt)
+
+        @pl.when((k >= 1) & (k < S - 1))
+        def _():
             relay(k + 1)
 
         t_reduce(src).wait_recv()
@@ -213,6 +232,8 @@
         return unused
 
     lax.fori_loop(0, S, chunk, jnp.int32(0))
+
+    relay(S)
 
     for i in range(S):
         keys_v[pl.ds(i * L, L), :] = kv[i, 0].T

time: 68.8 us -> 74.2 us (1.078)
  Pallas kernels: 64.7 us -> 70.1 us
    pallas_call x1, Pallas kernels: 64.7 us -> 70.1 us  [local(): pl.pallas_call(functools.partial(layer_kernel, (S, X, capp)), out_shape=(...]
where the time goes in v5:
time: 74.2 us; the launch traced here: 74 us
  Pallas kernels  70.1 us (94%)
  local copies, waits for them, and re-layouts  3.28 us (4%)
    pallas_call x1, Pallas kernels, local(): pl.pallas_call(functools.partial(layer_kernel, (S, X, capp)), out_shape=(...  70.1 us
    unnamed x2, local copies, waits for them, and re-layouts  3.28 us

profile of v5, /device:TPU:0, one launch (start us, length us, event | category | flops | bytes accessed | tf_op | source)
XLA Modules:
  0.0 74.0 jit_solution(4769281890277077254)
XLA Ops:
  0.6 70.1 %shard_map.140 = (bf16[288,256]{1,0:T(8,128)(2,1)}, bf16[128,1152]{1,0:T(8,128)(2,1)}) custom-call(bf16[288,256]{1,0:T(8,128)(2,1)} %bitcast.9, bf16[288,256]{1,0:T(8,128)(2,1)} %bitcast.10, bf16[288,256]{1,0:T(8,128)(2,1)} %bitcast.11, bf16[288,256]{1,0:T(8,128)(2,1)} %bitcast.12, bf16[288,256]{1,0:T(8,128)(2,1)} %bitcast.13, s32[2]{0:T(128)} %flags.1, ...), custom_call_target="tpu_custom_call" | custom-call | tf_op jit(solution)/shard_map/pallas_call | solution.py:319
  70.7 1.6 %copy.17 = bf16[256,288]{0,1:T(8,128)(2,1)} copy(bf16[256,288]{0,1:T(8,128)(2,1)} %bitcast.8) | data formatting | bytes 294912
  72.3 1.7 %copy.18 = bf16[128,1152]{1,0:T(8,128)(2,1)} copy(bf16[128,1152]{1,0:T(8,128)(2,1)} %get-tuple-element.9) | data formatting | bytes 589824

commit v6 on v5

--- a/solution.py
+++ b/solution.py
@@ -121,11 +121,13 @@
     rows[s, c, x] = slots_of(s)
     pl.semaphore_wait(barrier, S - 1 + X - 1 + 1)
     forward(s)
-    for j in range(S - 1):
+    def dispatch(j):
         e = remote(jnp.int32(j))
         disp[e] = slots_of(e)
         z_copy(e, s).start()
 
+    for j in range(min(2, S - 1)):
+        dispatch(j)
     for b in range(flags.shape[0]):
         fresh = flags[b] == 1
         part = pl.ds(b * blk, blk)
@@ -156,6 +158,8 @@
                 kv_copy(high, -1).start()
 
     relay(1)
+    for j in range(2, S - 1):
+        dispatch(j)
     nearest = order(jnp.int32(0))
     z_copy(nearest, nearest).wait_recv()
     forward(nearest)

time: 74.2 us -> 70.5 us (0.950)
  Pallas kernels: 70.1 us -> 66.4 us
    pallas_call x1, Pallas kernels: 70.1 us -> 66.4 us  [local(): pl.pallas_call(functools.partial(layer_kernel, (S, X, capp)), out_shape=(...]
where the time goes in v6:
time: 70.5 us; the launch traced here: 70.3 us
  Pallas kernels  66.4 us (94%)
  local copies, waits for them, and re-layouts  3.28 us (5%)
    pallas_call x1, Pallas kernels, local(): pl.pallas_call(functools.partial(layer_kernel, (S, X, capp)), out_shape=(...  66.4 us
    unnamed x2, local copies, waits for them, and re-layouts  3.28 us

profile of v6, /device:TPU:0, one launch (start us, length us, event | category | flops | bytes accessed | tf_op | source)
XLA Modules:
  0.0 70.3 jit_solution(842572006811748066)
XLA Ops:
  0.6 66.4 %shard_map.140 = (bf16[288,256]{1,0:T(8,128)(2,1)}, bf16[128,1152]{1,0:T(8,128)(2,1)}) custom-call(bf16[288,256]{1,0:T(8,128)(2,1)} %bitcast.9, bf16[288,256]{1,0:T(8,128)(2,1)} %bitcast.10, bf16[288,256]{1,0:T(8,128)(2,1)} %bitcast.11, bf16[288,256]{1,0:T(8,128)(2,1)} %bitcast.12, bf16[288,256]{1,0:T(8,128)(2,1)} %bitcast.13, s32[2]{0:T(128)} %flags.1, ...), custom_call_target="tpu_custom_call" | custom-call | tf_op jit(solution)/shard_map/pallas_call | solution.py:323
  67.0 1.6 %copy.17 = bf16[256,288]{0,1:T(8,128)(2,1)} copy(bf16[256,288]{0,1:T(8,128)(2,1)} %bitcast.8) | data formatting | bytes 294912
  68.6 1.7 %copy.18 = bf16[128,1152]{1,0:T(8,128)(2,1)} copy(bf16[128,1152]{1,0:T(8,128)(2,1)} %get-tuple-element.9) | data formatting | bytes 589824

commit v7 on v6

--- a/solution.py
+++ b/solution.py
@@ -223,9 +223,13 @@
             z_copy(nxt, nxt).wait_recv()
             forward(nxt)
 
-        @pl.when((k >= 1) & (k < S - 1))
-        def _():
-            relay(k + 1)
+        @pl.when((k == 1) & (k < S - 1))
+        def _():
+            relay(2)
+
+        @pl.when(k >= 3)
+        def _():
+            relay(k)
 
         t_reduce(src).wait_recv()
         for i in range(X):
@@ -237,6 +241,7 @@
 
     lax.fori_loop(0, S, chunk, jnp.int32(0))
 
+    finish_send(order(S - 1))
     relay(S)
 
     for i in range(S):
@@ -260,7 +265,6 @@
     acc[...] = jnp.zeros_like(acc)
     lax.fori_loop(0, heads, head, jnp.int32(0))
     attn_ref[...] = acc[...].astype(BF16)
-    finish_send(order(S - 1))
 
     base = jnp.where(named, place, 0.0) + (expert * capp).astype(F32)
     turn[...] = jnp.zeros_like(turn)

time: 70.5 us -> 74.2 us (1.052)
  Pallas kernels: 66.4 us -> 70.1 us
    pallas_call x1, Pallas kernels: 66.4 us -> 70.1 us  [local(): pl.pallas_call(functools.partial(layer_kernel, (S, X, capp)), out_shape=(...]
where the time goes in v7:
time: 74.2 us; the launch traced here: 74 us
  Pallas kernels  70.1 us (94%)
  local copies, waits for them, and re-layouts  3.28 us (4%)
    pallas_call x1, Pallas kernels, local(): pl.pallas_call(functools.partial(layer_kernel, (S, X, capp)), out_shape=(...  70.1 us
    unnamed x2, local copies, waits for them, and re-layouts  3.28 us

profile of v7, /device:TPU:0, one launch (start us, length us, event | category | flops | bytes accessed | tf_op | source)
XLA Modules:
  0.0 74.0 jit_solution(14089166125056431402)
XLA Ops:
  0.6 70.1 %shard_map.140 = (bf16[288,256]{1,0:T(8,128)(2,1)}, bf16[128,1152]{1,0:T(8,128)(2,1)}) custom-call(bf16[288,256]{1,0:T(8,128)(2,1)} %bitcast.9, bf16[288,256]{1,0:T(8,128)(2,1)} %bitcast.10, bf16[288,256]{1,0:T(8,128)(2,1)} %bitcast.11, bf16[288,256]{1,0:T(8,128)(2,1)} %bitcast.12, bf16[288,256]{1,0:T(8,128)(2,1)} %bitcast.13, s32[2]{0:T(128)} %flags.1, ...), custom_call_target="tpu_custom_call" | custom-call | tf_op jit(solution)/shard_map/pallas_call | solution.py:327
  70.7 1.6 %copy.17 = bf16[256,288]{0,1:T(8,128)(2,1)} copy(bf16[256,288]{0,1:T(8,128)(2,1)} %bitcast.8) | data formatting | bytes 294912
  72.3 1.7 %copy.18 = bf16[128,1152]{1,0:T(8,128)(2,1)} copy(bf16[128,1152]{1,0:T(8,128)(2,1)} %get-tuple-element.9) | data formatting | bytes 589824
